TPU v7x, 16 devices: a whole 2x2x2 slice. The times are simulated.
16 devices in a mesh: dp: 4 (over z, y), tp: 4 (over x, core).
Axes of the slice: x: 2, y: 2, z: 2, core: 2. Of those that a mesh axis runs over, the one named last changes fastest.
Arguments:
- hidden: bfloat16 [8, 512, 768], P('dp', None, 'tp'), parts along dimension 0
- ln_scale: float32 [768], P('tp')
- w_head: bfloat16 [768, 32128], P(None, 'tp')
- targets: int32 [8, 512], P('dp'), parts along dimension 0
- valid_mask: int32 [8, 512], P('dp'), parts along dimension 0
Outputs:
- output 1: float32 [8, 512], P('dp'), parts along dimension 0
- output 2: float32 [8], P('dp'), parts along dimension 0
There are 4 independent parts. A program takes and returns all parts, laid end to end along the dimension named above; an argument that names none is the same for every part.
All inputs are finite; a program needn't handle non-finite values.
Results may differ from a plain program's by a relative error of at most 0.001.
Values are sent between devices in bfloat16 or wider.
A program may use at most 1 GiB of HBM per device.

v0:
```python
import jax
import jax.numpy as jnp
from jax import lax
from jax.sharding import PartitionSpec as P, NamedSharding

NORM_EPS = 1e-6


def solution(mesh):
    tp_size = mesh.shape["tp"]

    def local_score(hidden, ln_scale, w_head, targets, valid_mask):
        d_local = hidden.shape[2]
        v_local = w_head.shape[1]
        row_f32 = hidden.astype(jnp.float32)
        sq_total = lax.psum(jnp.sum(row_f32 * row_f32, axis=-1), "tp")
        inv_rms = lax.rsqrt(sq_total / (d_local * tp_size) + NORM_EPS)
        normed = (row_f32 * inv_rms[..., None] * ln_scale).astype(jnp.bfloat16)
        full_rows = lax.all_gather(normed, "tp", axis=2, tiled=True)
        logits = jnp.einsum("bld,dv->blv", full_rows, w_head, preferred_element_type=jnp.float32)
        row_max = lax.pmax(jnp.max(logits, axis=-1), "tp")
        exp_sum = lax.psum(jnp.sum(jnp.exp(logits - row_max[..., None]), axis=-1), "tp")
        log_norm = row_max + jnp.log(exp_sum)
        local_idx = targets - lax.axis_index("tp") * v_local
        in_shard = (local_idx >= 0) & (local_idx < v_local)
        safe_idx = jnp.clip(local_idx, 0, v_local - 1)
        own_logit = jnp.take_along_axis(logits, safe_idx[..., None], axis=-1)[..., 0]
        picked = lax.psum(jnp.where(in_shard, own_logit, 0.0), "tp")
        token_logp = valid_mask.astype(jnp.float32) * (picked - log_norm)
        return token_logp, jnp.sum(token_logp, axis=1)

    return jax.shard_map(
        local_score,
        mesh=mesh,
        in_specs=(P("dp", None, "tp"), P("tp"), P(None, "tp"), P("dp", None), P("dp", None)),
        out_specs=(P("dp", None), P("dp")),
        check_vma=False,
    )
```

profile of v0, /device:TPU:0, one launch (start us, length us, event | category | flops | bytes accessed | tf_op | source)
XLA Modules:
  0.0 130.9 jit_solution(2854234500100135701)
XLA Ops:
  7.2 0.0 all-gather.2.cloned.1.call-start
  7.2 1.1 fusion.2
  8.3 8.6 %psum.21 = f32[2,512]{1,0:T(2,128)S(1)} all-reduce(f32[2,512]{1,0:T(2,128)S(1)} %fusion.2), channel_id=1, replica_groups=mesh['dp'=4,'tp'=4] {'tp'}, use_global_device_ids=true, to_apply=%region_1.0 | all-reduce | flops 1024 | bytes 8192 | tf_op jit(solution)/shard_map/psum | solution.py:16
  17.0 1.9 %fusion.4 = bf16[2,512,192]{1,2,0:T(8,128)(2,1)} fusion(bf16[2,512,192]{1,2,0:T(8,128)(2,1)} %param.5, f32[192]{0:T(256)} %param.6, f32[2,512]{1,0:T(2,128)S(1)} %add_rsqrt_fusion), kind=kLoop, calls=%fused_computation.8 | loop fusion | flops 786432 | bytes 791296 | tf_op jit(solution)/shard_map/convert_element_type | solution.py:18
  18.8 0.0 all-gather.2.cloned.1.call-update
  18.8 0.7 fusion.11
  19.6 17.1 %all-gather.2.cloned.1.call-done = bf16[2,512,768]{1,2,0:T(8,128)(2,1)} async-done(((bf16[2,512,192]{1,2,0:T(8,128)(2,1)}), bf16[2,512,768]{1,2,0:T(8,128)(2,1)}) %all-gather.2.cloned.1.call-update) | async-done | bytes 1572880 | tf_op jit(solution)/shard_map/all_gather | solution.py:19
  36.7 22.1 %fusion.13 = (f32[2,512]{1,0:T(2,128)S(1)}, f32[2,512,8032]{1,2,0:T(8,128)}) fusion(bf16[2,512,768]{1,2,0:T(8,128)(2,1)} %all-gather.2.cloned.1.call-done, bf16[768,8032]{0,1:T(8,128)(2,1)} %param.7), kind=kOutput, calls=%fused_computation.26 | convolution fusion | flops 12641467392 | bytes 46813184 | tf_op jit(solution)/shard_map/bld,dv->blv/dot_general | solution.py:20
  58.8 5.9 %pmax.7 = f32[2,512]{1,0:T(2,128)S(1)} all-reduce(f32[2,512]{1,0:T(2,128)S(1)} %get-tuple-element.6), channel_id=1, replica_groups=mesh['dp'=4,'tp'=4] {'tp'}, use_global_device_ids=true, to_apply=%region_4.0 | all-reduce | flops 1024 | bytes 8192 | tf_op jit(solution)/shard_map/pmax | solution.py:21
  64.6 0.0 copy-start
  64.6 0.0 copy-start.1
  64.6 14.9 %exponential_reduce_fusion = f32[2,512]{1,0:T(2,128)S(1)} fusion(f32[2,512,8032]{1,2,0:T(8,128)} %get-tuple-element.7, f32[2,512]{1,0:T(2,128)S(1)} %pmax.7), kind=kLoop, calls=%fused_computation.1 | loop fusion | flops 16448512 | bytes 32907264 | tf_op jit(solution)/shard_map/reduce_sum | solution.py:22
  79.5 37.4 %gather_fusion = f32[1024]{0:T(1024)S(1)} fusion(f32[2,512,8032]{1,2,0:T(8,128)} %get-tuple-element.7, s32[1024]{0:T(1024)S(1)} %bitcast.14), kind=kCustom, calls=%fused_computation | custom fusion | bytes 20480 | tf_op jit(solution)/shard_map/jit(take_along_axis)/gather | solution.py:27
  116.9 0.0 copy-done
  116.9 5.9 %all-reduce = (f32[2,512]{1,0:T(2,128)S(1)}, f32[2,512]{1,0:T(2,128)S(1)}) all-reduce(f32[2,512]{1,0:T(2,128)S(1)} %and_select_fusion.1, f32[2,512]{1,0:T(2,128)S(1)} %exponential_reduce_fusion), channel_id=1, replica_groups=mesh['dp'=4,'tp'=4] {'tp'}, use_global_device_ids=true, to_apply=%region_2.0 | all-reduce | flops 2048 | bytes 16384 | tf_op jit(solution)/shard_map/psum | solution.py:28
  122.8 0.0 copy-done.1
  122.8 1.2 fusion.12
  (8 shorter events, 0.1 us)
Async XLA Ops:
  7.2 29.5 %all-gather.2.cloned.1.call-start = ((), (), s32[]{:S(2)}) async-start(), calls=%async_computation | async-start | bytes 1966080 | tf_op jit(solution)/shard_map/all_gather | solution.py:19
  64.6 52.3 %copy-start = (s32[2,512]{1,0:T(2,128)S(1)}, s32[2,512]{1,0:T(2,128)}, u32[]{:S(2)}) copy-start(s32[2,512]{1,0:T(2,128)} %param.8) | copy-start | bytes 12292
  64.6 58.2 %copy-start.1 = (s32[2,512]{1,0:T(2,128)S(1)}, s32[2,512]{1,0:T(2,128)}, u32[]{:S(2)}) copy-start(s32[2,512]{1,0:T(2,128)} %param.9) | copy-start | bytes 12292
Sparse Core Ops, SparseCore 0:
  19.0 17.6 all-gather.1
where the time goes:
time: 132 us; the launch traced here: 131 us
  local copies, waits for them, and re-layouts  37.4 us (28%)
  matrix products  22.1 us (17%)
  blocking collectives  20.4 us (15%)
  other arithmetic  19.8 us (15%)
  waiting for transfers between devices  17.1 us (13%)
  between operations  14.1 us (11%)
    gather x2, local copies, waits for them, and re-layouts, local_score(): jnp.take_along_axis(logits, safe_idx[..., None], axis=-1)[..., 0]  37.4 us
    dot_general x1, matrix products, local_score(): jnp.einsum('bld,dv->blv', full_rows, w_head, preferred_element_type=jnp.f...  22.1 us
    all_gather x1, waiting for transfers between devices, local_score(): full_rows = lax.all_gather(normed, 'tp', axis=2, tiled=True)  17.1 us
    reduce_sum x1, other arithmetic, local_score(): jnp.sum(jnp.exp(logits - row_max[..., None]), axis=-1)  14.9 us
    psum x1, blocking collectives, local_score(): sq_total = lax.psum(jnp.sum(row_f32 * row_f32, axis=-1), 'tp')  8.64 us
    psum x1, blocking collectives, local_score(): picked = lax.psum(jnp.where(in_shard, own_logit, 0.0), 'tp')  5.87 us
    pmax x1, blocking collectives, local_score(): row_max = lax.pmax(jnp.max(logits, axis=-1), 'tp')  5.86 us
  transfers between devices with their start and end apart: 1, of which 1 were waited for; matrix products, arithmetic and copies ran while one was open for 1% of the time, Pallas kernels for 0%

commit v1 on v0

v1 whole, which is shorter than its diff:
```python
import functools

import jax
import jax.numpy as jnp
from jax import lax
from jax.experimental import pallas as pl
from jax.experimental.pallas import tpu as pltpu
from jax.sharding import PartitionSpec as P

NORM_EPS = 1e-6
LOG2E = 1.4426950408889634
MESH = pl.DeviceIdType.MESH
LANES = 128


def head_kernel(
    cfg, h_ref, g_ref, w_ref, tgt_ref, out_ref,
    wbuf, hrx, grx, tbuf, gcol, xbuf, zbuf, stx, srx,
    w_sem, own_sem, small_sem, psend, precv, xsend, xrecv, fsend, frecv, gsend, grecv, ssend, srecv,
):
    d_local, v_local, rows, chunk, block = cfg
    n_chunks = rows // chunk
    d_full = 4 * d_local
    per_seq = h_ref.shape[2]
    per_chunk = per_seq // chunk
    starts = list(range(0, v_local, block))
    n_blocks = len(starts)

    me = lax.axis_index("tp")
    peer = me + 1 - 2 * lax.rem(me, 2)
    cross = lax.rem(me + 2, 4)
    diag = lax.rem(peer + 2, 4)
    others = (peer, cross, diag)

    def piece(owner, k):
        return hrx.at[k, pl.ds(pl.multiple_of(owner * d_local, d_local), d_local)]

    own = [
        pltpu.make_async_copy(
            h_ref.at[k // per_chunk, :, pl.ds((k % per_chunk) * chunk, chunk)], piece(me, k), own_sem.at[k]
        )
        for k in range(n_chunks)
    ]
    own_g = pltpu.make_async_copy(g_ref, grx.at[me], small_sem.at[0])
    own_t = pltpu.make_async_copy(tgt_ref, tbuf, small_sem.at[1])
    load_w = pltpu.make_async_copy(w_ref, wbuf, w_sem)
    own[0].start()
    own_g.start()
    own_t.start()
    for k in range(1, n_chunks):
        own[k].start()
    load_w.start()

    barrier = pltpu.get_barrier_semaphore()
    for other in others:
        pl.semaphore_signal(barrier, inc=1, device_id={"tp": other}, device_id_type=MESH)
    pl.semaphore_wait(barrier, 3)

    def remote(src, dst, send, recv, dev):
        return pltpu.make_async_remote_copy(
            src_ref=src, dst_ref=dst, send_sem=send, recv_sem=recv, device_id={"tp": dev}, device_id_type=MESH
        )

    def cross_copy(k):
        return remote(piece(me, k), piece(me, k), xsend.at[k], xrecv.at[k], cross)

    def peer_copy(k):
        return remote(piece(me, k), piece(me, k), psend.at[k], precv.at[k], peer)

    def forward_copy(k):
        return remote(piece(cross, k), piece(cross, k), fsend.at[k], frecv.at[k], peer)

    def gain_copy(n):
        return remote(grx.at[me], grx.at[me], gsend.at[n], grecv.at[n], others[n])

    def stat_copy(n, k):
        return remote(stx.at[k], srx.at[n, k], ssend.at[n, k], srecv.at[n, k], others[n])

    own[0].wait()
    cross_copy(0).start()
    peer_copy(0).start()
    own_g.wait()
    for n in range(3):
        gain_copy(n).start()
    for k in range(1, n_chunks):
        own[k].wait()
        cross_copy(k).start()
        peer_copy(k).start()
    own_t.wait()

    for n in range(3):
        gain_copy(n).wait_recv()
    for s in range(4):
        for lo in range(0, d_local, LANES):
            size = min(LANES, d_local - lo)
            row = grx[s, :, lo : lo + size]
            row = jnp.concatenate([row] * (LANES // size), axis=-1)
            gcol[s * d_local + lo : s * d_local + lo + size, :] = jnp.broadcast_to(row, (LANES, LANES)).T[0:size]

    group = 32

    def normalise(k, slot):
        def square(i, acc):
            at = pl.ds(pl.multiple_of(i * group, group), group)
            part = hrx[k, at, :].astype(jnp.float32)
            return acc + part * part

        sq = lax.fori_loop(0, d_full // group, square, jnp.zeros((group, chunk), jnp.float32), unroll=True)
        inv = lax.rsqrt(jnp.sum(sq, axis=0, keepdims=True) / d_full + NORM_EPS)

        def scale(i, carry):
            at = pl.ds(pl.multiple_of(i * group, group), group)
            gain = gcol[at, :]
            part = hrx[k, at, :].astype(jnp.float32)
            gains = jnp.concatenate([gain] * (chunk // LANES), axis=-1)
            xbuf[slot, at, :] = (part * inv * gains).astype(jnp.bfloat16)
            return carry

        lax.fori_loop(0, d_full // group, scale, 0, unroll=True)

    sub = lax.broadcasted_iota(jnp.int32, (8, chunk), 0)

    def logits(j, xslot, zslot):
        lo = starts[j]
        size = min(block, v_local - lo)
        z = jnp.dot(wbuf[lo : lo + size, :], xbuf[xslot], preferred_element_type=jnp.float32)
        zbuf[zslot, 0:size, :] = z

    def epilogue(j, zslot, want, state):
        lo = starts[j]
        size = min(block, v_local - lo)

        def tile(i):
            return zbuf[zslot, pl.ds(pl.multiple_of(i * 8, 8), 8), :]

        top = lax.fori_loop(1, size // 8, lambda i, t: jnp.maximum(t, tile(i)), tile(0), unroll=True)
        if state is None:
            total = jnp.zeros((8, chunk), jnp.float32)
            pick = total
        else:
            old, total, pick = state
            top = jnp.maximum(top, old)
            total = total * jnp.exp2((old - top) * LOG2E)

        def add(i, carry):
            total, pick = carry
            z = tile(i)
            total = total + jnp.exp2((z - top) * LOG2E)
            pick = jnp.where(want == lo + i * 8, z, pick)
            return total, pick

        total, pick = lax.fori_loop(0, size // 8, add, (total, pick), unroll=True)
        return top, total, pick

    def finish_chunk(k, state):
        m, total, pick = state
        top = jnp.max(m, axis=0, keepdims=True)
        stx[k, 0:1, :] = top
        stx[k, 1:2, :] = jnp.sum(total * jnp.exp2((m - top) * LOG2E), axis=0, keepdims=True)
        stx[k, 2:3, :] = jnp.sum(pick, axis=0, keepdims=True)

    cross_copy(0).wait_recv()
    forward_copy(0).start()
    peer_copy(0).wait_recv()
    forward_copy(0).wait_recv()
    normalise(0, 0)
    load_w.wait()

    half = n_blocks // 2

    def step(k, carry):
        xslot = lax.rem(k, 2)
        row = tbuf[pl.ds(k // per_chunk, 1), pl.ds(pl.multiple_of(lax.rem(k, per_chunk) * chunk, chunk), chunk)]
        local = row - me * v_local
        local = jnp.where((local >= 0) & (local < v_local), local, jnp.int32(-(1 << 20)))
        want = jnp.broadcast_to(local, (8, chunk)) - sub
        state = None
        for j in range(n_blocks):
            if j == half:
                @pl.when(k < n_chunks - 1)
                def _():
                    cross_copy(k + 1).wait_recv()
                    forward_copy(k + 1).start()

            if j == n_blocks - 1:
                @pl.when(k < n_chunks - 1)
                def _():
                    peer_copy(k + 1).wait_recv()
                    forward_copy(k + 1).wait_recv()

            logits(j, xslot, j % 2)
            if j:
                state = epilogue(j - 1, (j - 1) % 2, want, state)
            if j == n_blocks - 1:
                normalise(lax.min(k + 1, n_chunks - 1), 1 - xslot)
        state = epilogue(n_blocks - 1, (n_blocks - 1) % 2, want, state)
        finish_chunk(k, state)
        for n in range(3):
            stat_copy(n, k).start()
        return carry

    lax.fori_loop(0, n_chunks, step, 0)

    for k in range(n_chunks):
        for n in range(3):
            stat_copy(n, k).wait_recv()
        stats = [stx[k]] + [srx[n, k] for n in range(3)]
        top = stats[0][0:1]
        for st in stats[1:]:
            top = jnp.maximum(top, st[0:1])
        total = jnp.zeros_like(top)
        pick = jnp.zeros_like(top)
        for st in stats:
            total = total + st[1:2] * jnp.exp2((st[0:1] - top) * LOG2E)
            pick = pick + st[2:3]
        seq, pos = divmod(k * chunk, per_seq)
        out_ref[seq : seq + 1, pos : pos + chunk] = pick - (top + jnp.log(total))

    for k in range(n_chunks):
        cross_copy(k).wait_send()
        peer_copy(k).wait_send()
        forward_copy(k).wait_send()
        for n in range(3):
            stat_copy(n, k).wait_send()
    for n in range(3):
        gain_copy(n).wait_send()


def solution(mesh):
    def local_score(hidden, ln_scale, w_head, targets, valid_mask):
        b, l, d_local = hidden.shape
        v_local = w_head.shape[1]
        rows, chunk, block = b * l, 256, 512
        n_chunks = rows // chunk
        any_spec = pl.BlockSpec(memory_space=pl.ANY)
        f32 = jnp.float32
        dma = pltpu.SemaphoreType.DMA
        token = pl.pallas_call(
            functools.partial(head_kernel, (d_local, v_local, rows, chunk, block)),
            out_shape=jax.ShapeDtypeStruct((b, l), f32),
            in_specs=[any_spec] * 4,
            out_specs=pl.BlockSpec(memory_space=pltpu.VMEM),
            scratch_shapes=[
                pltpu.VMEM((v_local, 4 * d_local), jnp.bfloat16),
                pltpu.VMEM((n_chunks, 4 * d_local, chunk), jnp.bfloat16),
                pltpu.VMEM((4, 1, d_local), f32),
                pltpu.VMEM((b, l), jnp.int32),
                pltpu.VMEM((4 * d_local, LANES), f32),
                pltpu.VMEM((2, 4 * d_local, chunk), jnp.bfloat16),
                pltpu.VMEM((2, block, chunk), f32),
                pltpu.VMEM((n_chunks, 8, chunk), f32),
                pltpu.VMEM((3, n_chunks, 8, chunk), f32),
                dma,
                dma((n_chunks,)),
                dma((2,)),
                dma((n_chunks,)), dma((n_chunks,)),
                dma((n_chunks,)), dma((n_chunks,)),
                dma((n_chunks,)), dma((n_chunks,)),
                dma((3,)), dma((3,)),
                dma((3, n_chunks)), dma((3, n_chunks)),
            ],
            compiler_params=pltpu.CompilerParams(
                collective_id=0, has_side_effects=True, vmem_limit_bytes=62 * 1024 * 1024
            ),
        )(hidden.transpose(0, 2, 1), ln_scale.reshape(1, d_local), w_head.T, targets)
        token_logp = valid_mask.astype(f32) * token
        return token_logp, jnp.sum(token_logp, axis=1)

    return jax.shard_map(
        local_score,
        mesh=mesh,
        in_specs=(P("dp", None, "tp"), P("tp"), P(None, "tp"), P("dp", None), P("dp", None)),
        out_specs=(P("dp", None), P("dp")),
        check_vma=False,
    )
```

time: 132 us -> 35.2 us (0.27)
  local copies, waits for them, and re-layouts: 37.4 us -> 0.01 us
  Pallas kernels: 0 us -> 32.5 us
  matrix products: 22.1 us -> 0 us
  blocking collectives: 20.4 us -> 0 us
  other arithmetic: 19.8 us -> 1.9 us
  waiting for transfers between devices: 17.1 us -> 0 us
  between operations: 14.1 us -> 0.65 us
    gather x2 -> x0, local copies, waits for them, and re-layouts: 37.4 us -> none  [local_score(): jnp.take_along_axis(logits, safe_idx[..., None], axis=-1)[..., 0]]
    pallas_call x0 -> x1, Pallas kernels: none -> 32.5 us  [local_score(): pl.pallas_call(functools.partial(head_kernel, (d_local, v_local, rows, ch...]
    dot_general x1 -> x0, matrix products: 22.1 us -> none  [local_score(): jnp.einsum('bld,dv->blv', full_rows, w_head, preferred_element_type=jnp.f...]
    all_gather x1 -> x0, waiting for transfers between devices: 17.1 us -> none  [local_score(): full_rows = lax.all_gather(normed, 'tp', axis=2, tiled=True)]
    reduce_sum x2 -> x0, other arithmetic: 16 us -> none  [the longest x1 14.9 us: local_score(): jnp.sum(jnp.exp(logits - row_max[..., None]), axis=-1)]
    psum x2 -> x0, blocking collectives: 14.5 us -> none  [the longest x1 8.64 us: local_score(): sq_total = lax.psum(jnp.sum(row_f32 * row_f32, axis=-1), 'tp')]
    pmax x1 -> x0, blocking collectives: 5.86 us -> none  [local_score(): row_max = lax.pmax(jnp.max(logits, axis=-1), 'tp')]
    convert_element_type x1 -> x0, other arithmetic: 1.85 us -> none  [local_score(): normed = (row_f32 * inv_rms[..., None] * ln_scale).astype(jnp.bfloat16)]
  transfers between devices with their start and end apart: 1 -> 0, of which waited for: 1 -> 0; matrix products, arithmetic and copies ran while one was open for 1% -> 0% of each run, Pallas kernels for 0% -> 0%
where the time goes in v1:
time: 35.2 us; the launch traced here: 35.1 us
  Pallas kernels  32.5 us (92%)
  other arithmetic  1.9 us (5%)
  between operations  0.65 us (2%)
    pallas_call x1, Pallas kernels, local_score(): pl.pallas_call(functools.partial(head_kernel, (d_local, v_local, rows, ch...  32.5 us
    reduce_sum x1, other arithmetic, local_score(): return (token_logp, jnp.sum(token_logp, axis=1))  1.9 us

profile of v1, /device:TPU:0, one launch (start us, length us, event | category | flops | bytes accessed | tf_op | source)
XLA Modules:
  0.0 35.1 jit_solution(9562182804200065470)
XLA Ops:
  0.6 0.0 copy-start
  0.6 32.5 %shard_map.68 = f32[2,512]{1,0:T(2,128)} custom-call(bf16[2,192,512]{2,1,0:T(8,128)(2,1)} %bitcast.4, f32[1,192]{1,0:T(1,128)} %bitcast.5, bf16[8032,768]{1,0:T(8,128)(2,1)} %bitcast.3, s32[2,512]{1,0:T(2,128)} %tgt_ref.1), custom_call_target="tpu_custom_call" | custom-call | tf_op jit(solution)/shard_map/pallas_call | solution.py:238
  33.2 0.0 copy-done
  33.2 1.9 %fusion = (f32[2]{0:T(128)}, f32[2,512]{1,0:T(2,128)}) fusion(f32[2,512]{1,0:T(2,128)} %shard_map.68, s32[2,512]{1,0:T(2,128)S(1)} %copy-done), kind=kLoop, calls=%fused_computation.1 | loop fusion | flops 3070 | bytes 12296 | tf_op jit(solution)/shard_map/reduce_sum | solution.py:267
Async XLA Ops:
  0.6 32.5 %copy-start = (s32[2,512]{1,0:T(2,128)S(1)}, s32[2,512]{1,0:T(2,128)}, u32[]{:S(2)}) copy-start(s32[2,512]{1,0:T(2,128)} %param.9) | copy-start | bytes 12292

commit v2 on v1

--- a/solution.py
+++ b/solution.py
@@ -44,11 +44,10 @@
     own_g = pltpu.make_async_copy(g_ref, grx.at[me], small_sem.at[0])
     own_t = pltpu.make_async_copy(tgt_ref, tbuf, small_sem.at[1])
     load_w = pltpu.make_async_copy(w_ref, wbuf, w_sem)
-    own[0].start()
     own_g.start()
+    for k in range(n_chunks):
+        own[k].start()
     own_t.start()
-    for k in range(1, n_chunks):
-        own[k].start()
     load_w.start()
 
     barrier = pltpu.get_barrier_semaphore()
@@ -76,13 +75,10 @@
     def stat_copy(n, k):
         return remote(stx.at[k], srx.at[n, k], ssend.at[n, k], srecv.at[n, k], others[n])
 
-    own[0].wait()
-    cross_copy(0).start()
-    peer_copy(0).start()
     own_g.wait()
     for n in range(3):
         gain_copy(n).start()
-    for k in range(1, n_chunks):
+    for k in range(n_chunks):
         own[k].wait()
         cross_copy(k).start()
         peer_copy(k).start()
@@ -260,9 +256,12 @@
                 dma((3, n_chunks)), dma((3, n_chunks)),
             ],
             compiler_params=pltpu.CompilerParams(
-                collective_id=0, has_side_effects=True, vmem_limit_bytes=62 * 1024 * 1024
+                collective_id=0, has_side_effects=True, vmem_limit_bytes=40 * 1024 * 1024
             ),
-        )(hidden.transpose(0, 2, 1), ln_scale.reshape(1, d_local), w_head.T, targets)
+        )(*[
+            pltpu.with_memory_space_constraint(x, pltpu.HBM)
+            for x in (hidden.transpose(0, 2, 1), ln_scale.reshape(1, d_local), w_head.T, targets)
+        ])
         token_logp = valid_mask.astype(f32) * token
         return token_logp, jnp.sum(token_logp, axis=1)
 

time: 35.2 us -> 33.3 us (0.946)
  Pallas kernels: 32.5 us -> 31.3 us
  other arithmetic: 1.9 us -> 1.22 us
    pallas_call x1, Pallas kernels: 32.5 us -> 31.3 us  [local_score(): pl.pallas_call(functools.partial(head_kernel, (d_local, v_local, rows, ch...]
    reduce_sum x1, other arithmetic: 1.9 us -> 1.22 us  [local_score(): return (token_logp, jnp.sum(token_logp, axis=1))]
where the time goes in v2:
time: 33.3 us; the launch traced here: 33.2 us
  Pallas kernels  31.3 us (94%)
  other arithmetic  1.22 us (4%)
  between operations  0.65 us (2%)
    pallas_call x1, Pallas kernels, local_score(): pl.pallas_call(functools.partial(head_kernel, (d_local, v_local, rows, ch...  31.3 us
    reduce_sum x1, other arithmetic, local_score(): return (token_logp, jnp.sum(token_logp, axis=1))  1.22 us

profile of v2, /device:TPU:0, one launch (start us, length us, event | category | flops | bytes accessed | tf_op | source)
XLA Modules:
  0.0 33.2 jit_solution(6797641066702488520)
XLA Ops:
  0.6 0.0 copy-start
  0.6 31.3 %shard_map.68 = f32[2,512]{1,0:T(2,128)S(1)} custom-call(bf16[2,192,512]{2,1,0:T(8,128)(2,1)} %bitcast.4, f32[1,192]{1,0:T(1,128)} %bitcast.5, bf16[8032,768]{1,0:T(8,128)(2,1)} %bitcast.3, s32[2,512]{1,0:T(2,128)} %tgt_ref.1), custom_call_target="tpu_custom_call" | custom-call | tf_op jit(solution)/shard_map/pallas_call | solution.py:234
  32.0 0.0 copy-done
  32.0 1.2 %fusion = (f32[2]{0:T(128)}, f32[2,512]{1,0:T(2,128)}) fusion(f32[2,512]{1,0:T(2,128)S(1)} %shard_map.68, s32[2,512]{1,0:T(2,128)S(1)} %copy-done), kind=kLoop, calls=%fused_computation.1 | loop fusion | flops 3070 | bytes 12296 | tf_op jit(solution)/shard_map/reduce_sum | solution.py:266
Async XLA Ops:
  0.6 31.3 %copy-start = (s32[2,512]{1,0:T(2,128)S(1)}, s32[2,512]{1,0:T(2,128)}, u32[]{:S(2)}) copy-start(s32[2,512]{1,0:T(2,128)} %param.9) | copy-start | bytes 12292

commit v3 on v2

--- a/solution.py
+++ b/solution.py
@@ -18,7 +18,7 @@
     wbuf, hrx, grx, tbuf, gcol, xbuf, zbuf, stx, srx,
     w_sem, own_sem, small_sem, psend, precv, xsend, xrecv, fsend, frecv, gsend, grecv, ssend, srecv,
 ):
-    d_local, v_local, rows, chunk, block = cfg
+    d_local, v_local, rows, chunk, block, w_parts = cfg
     n_chunks = rows // chunk
     d_full = 4 * d_local
     per_seq = h_ref.shape[2]
@@ -43,12 +43,14 @@
     ]
     own_g = pltpu.make_async_copy(g_ref, grx.at[me], small_sem.at[0])
     own_t = pltpu.make_async_copy(tgt_ref, tbuf, small_sem.at[1])
-    load_w = pltpu.make_async_copy(w_ref, wbuf, w_sem)
+    load_w = [
+        pltpu.make_async_copy(w_ref.at[pl.ds(lo, size)], wbuf.at[pl.ds(lo, size)], w_sem.at[n])
+        for n, (lo, size) in enumerate(w_parts)
+    ]
     own_g.start()
     for k in range(n_chunks):
         own[k].start()
     own_t.start()
-    load_w.start()
 
     barrier = pltpu.get_barrier_semaphore()
     for other in others:
@@ -82,6 +84,10 @@
         own[k].wait()
         cross_copy(k).start()
         peer_copy(k).start()
+        if k == 1:
+            load_w[0].start()
+    for part in load_w[1:]:
+        part.start()
     own_t.wait()
 
     for n in range(3):
@@ -160,7 +166,8 @@
     peer_copy(0).wait_recv()
     forward_copy(0).wait_recv()
     normalise(0, 0)
-    load_w.wait()
+    for part in load_w:
+        part.wait()
 
     half = n_blocks // 2
 
@@ -227,12 +234,14 @@
         b, l, d_local = hidden.shape
         v_local = w_head.shape[1]
         rows, chunk, block = b * l, 256, 512
+        part = 2048
+        w_parts = tuple((lo, min(part, v_local - lo)) for lo in range(0, v_local, part))
         n_chunks = rows // chunk
         any_spec = pl.BlockSpec(memory_space=pl.ANY)
         f32 = jnp.float32
         dma = pltpu.SemaphoreType.DMA
         token = pl.pallas_call(
-            functools.partial(head_kernel, (d_local, v_local, rows, chunk, block)),
+            functools.partial(head_kernel, (d_local, v_local, rows, chunk, block, w_parts)),
             out_shape=jax.ShapeDtypeStruct((b, l), f32),
             in_specs=[any_spec] * 4,
             out_specs=pl.BlockSpec(memory_space=pltpu.VMEM),
@@ -246,7 +255,7 @@
                 pltpu.VMEM((2, block, chunk), f32),
                 pltpu.VMEM((n_chunks, 8, chunk), f32),
                 pltpu.VMEM((3, n_chunks, 8, chunk), f32),
-                dma,
+                dma((len(w_parts),)),
                 dma((n_chunks,)),
                 dma((2,)),
                 dma((n_chunks,)), dma((n_chunks,)),

time: 33.3 us -> 31.4 us (0.943)
  Pallas kernels: 31.3 us -> 29.4 us
    pallas_call x1, Pallas kernels: 31.3 us -> 29.4 us  [local_score(): pl.pallas_call(functools.partial(head_kernel, (d_local, v_local, rows, ch...]
where the time goes in v3:
time: 31.4 us; the launch traced here: 31.3 us
  Pallas kernels  29.4 us (94%)
  other arithmetic  1.22 us (4%)
  between operations  0.65 us (2%)
    pallas_call x1, Pallas kernels, local_score(): pl.pallas_call(functools.partial(head_kernel, (d_local, v_local, rows, ch...  29.4 us
    reduce_sum x1, other arithmetic, local_score(): return (token_logp, jnp.sum(token_logp, axis=1))  1.22 us

profile of v3, /device:TPU:0, one launch (start us, length us, event | category | flops | bytes accessed | tf_op | source)
XLA Modules:
  0.0 31.3 jit_solution(8695582305762927888)
XLA Ops:
  0.6 0.0 copy-start
  0.6 29.4 %shard_map.68 = f32[2,512]{1,0:T(2,128)S(1)} custom-call(bf16[2,192,512]{2,1,0:T(8,128)(2,1)} %bitcast.4, f32[1,192]{1,0:T(1,128)} %bitcast.5, bf16[8032,768]{1,0:T(8,128)(2,1)} %bitcast.3, s32[2,512]{1,0:T(2,128)} %tgt_ref.1), custom_call_target="tpu_custom_call" | custom-call | tf_op jit(solution)/shard_map/pallas_call | solution.py:243
  30.1 0.0 copy-done
  30.1 1.2 %fusion = (f32[2]{0:T(128)}, f32[2,512]{1,0:T(2,128)}) fusion(f32[2,512]{1,0:T(2,128)S(1)} %shard_map.68, s32[2,512]{1,0:T(2,128)S(1)} %copy-done), kind=kLoop, calls=%fused_computation.1 | loop fusion | flops 3070 | bytes 12296 | tf_op jit(solution)/shard_map/reduce_sum | solution.py:275
Async XLA Ops:
  0.6 29.4 %copy-start = (s32[2,512]{1,0:T(2,128)S(1)}, s32[2,512]{1,0:T(2,128)}, u32[]{:S(2)}) copy-start(s32[2,512]{1,0:T(2,128)} %param.9) | copy-start | bytes 12292

commit v4 on v3

--- a/solution.py
+++ b/solution.py
@@ -68,8 +68,11 @@
     def peer_copy(k):
         return remote(piece(me, k), piece(me, k), psend.at[k], precv.at[k], peer)
 
-    def forward_copy(k):
-        return remote(piece(cross, k), piece(cross, k), fsend.at[k], frecv.at[k], peer)
+    def diag_copy(k):
+        return remote(piece(me, k), piece(me, k), fsend.at[k], frecv.at[k], diag)
+
+    def forward_copy():
+        return remote(piece(cross, 0), piece(cross, 0), fsend.at[0], frecv.at[0], peer)
 
     def gain_copy(n):
         return remote(grx.at[me], grx.at[me], gsend.at[n], grecv.at[n], others[n])
@@ -77,18 +80,20 @@
     def stat_copy(n, k):
         return remote(stx.at[k], srx.at[n, k], ssend.at[n, k], srecv.at[n, k], others[n])
 
-    own_g.wait()
-    for n in range(3):
-        gain_copy(n).start()
-    for k in range(n_chunks):
-        own[k].wait()
-        cross_copy(k).start()
-        peer_copy(k).start()
-        if k == 1:
-            load_w[0].start()
-    for part in load_w[1:]:
-        part.start()
-    own_t.wait()
+    ns = jax.named_scope
+    with ns("own"):
+        own_g.wait()
+        for n in range(3):
+            gain_copy(n).start()
+        for k in range(n_chunks):
+            own[k].wait()
+            cross_copy(k).start()
+            peer_copy(k).start()
+            if k:
+                diag_copy(k).start()
+        for part in load_w:
+            part.start()
+        own_t.wait()
 
     for n in range(3):
         gain_copy(n).wait_recv()
@@ -101,7 +106,7 @@
 
     group = 32
 
-    def normalise(k, slot):
+    def normalise(k):
         def square(i, acc):
             at = pl.ds(pl.multiple_of(i * group, group), group)
             part = hrx[k, at, :].astype(jnp.float32)
@@ -115,25 +120,24 @@
             gain = gcol[at, :]
             part = hrx[k, at, :].astype(jnp.float32)
             gains = jnp.concatenate([gain] * (chunk // LANES), axis=-1)
-            xbuf[slot, at, :] = (part * inv * gains).astype(jnp.bfloat16)
+            xbuf[at, :] = (part * inv * gains).astype(jnp.bfloat16)
             return carry
 
         lax.fori_loop(0, d_full // group, scale, 0, unroll=True)
 
     sub = lax.broadcasted_iota(jnp.int32, (8, chunk), 0)
 
-    def logits(j, xslot, zslot):
+    def logits(j):
         lo = starts[j]
         size = min(block, v_local - lo)
-        z = jnp.dot(wbuf[lo : lo + size, :], xbuf[xslot], preferred_element_type=jnp.float32)
-        zbuf[zslot, 0:size, :] = z
-
-    def epilogue(j, zslot, want, state):
+        zbuf[j % 2, 0:size, :] = jnp.dot(wbuf[lo : lo + size, :], xbuf[...], preferred_element_type=jnp.float32)
+
+    def epilogue(j, want, state):
         lo = starts[j]
         size = min(block, v_local - lo)
 
         def tile(i):
-            return zbuf[zslot, pl.ds(pl.multiple_of(i * 8, 8), 8), :]
+            return zbuf[j % 2, pl.ds(pl.multiple_of(i * 8, 8), 8), :]
 
         top = lax.fori_loop(1, size // 8, lambda i, t: jnp.maximum(t, tile(i)), tile(0), unroll=True)
         if state is None:
@@ -161,52 +165,64 @@
         stx[k, 1:2, :] = jnp.sum(total * jnp.exp2((m - top) * LOG2E), axis=0, keepdims=True)
         stx[k, 2:3, :] = jnp.sum(pick, axis=0, keepdims=True)
 
-    cross_copy(0).wait_recv()
-    forward_copy(0).start()
-    peer_copy(0).wait_recv()
-    forward_copy(0).wait_recv()
-    normalise(0, 0)
-    for part in load_w:
-        part.wait()
-
-    half = n_blocks // 2
-
-    def step(k, carry):
-        xslot = lax.rem(k, 2)
+    with ns("cross0"):
+        cross_copy(0).wait_recv()
+    forward_copy().start()
+    with ns("fwd0"):
+        peer_copy(0).wait_recv()
+        forward_copy().wait_recv()
+    with ns("wwait"):
+        for part in load_w:
+            part.wait()
+
+    def targets_of(k):
         row = tbuf[pl.ds(k // per_chunk, 1), pl.ds(pl.multiple_of(lax.rem(k, per_chunk) * chunk, chunk), chunk)]
         local = row - me * v_local
         local = jnp.where((local >= 0) & (local < v_local), local, jnp.int32(-(1 << 20)))
-        want = jnp.broadcast_to(local, (8, chunk)) - sub
+        return jnp.broadcast_to(local, (8, chunk)) - sub
+
+    final = n_blocks - 1
+
+    def send_stats(k):
+        for n in range(3):
+            stat_copy(n, k).start()
+
+    def step(k, carry):
+        @pl.when(k > 0)
+        def _():
+            with ns("chunkwait"):
+                cross_copy(k).wait_recv()
+                peer_copy(k).wait_recv()
+                diag_copy(k).wait_recv()
+
+        @pl.when(k > 1)
+        def _():
+            send_stats(k - 2)
+
+        normalise(k)
+        last_want, *last_state = carry
+        want = targets_of(k)
         state = None
         for j in range(n_blocks):
-            if j == half:
-                @pl.when(k < n_chunks - 1)
-                def _():
-                    cross_copy(k + 1).wait_recv()
-                    forward_copy(k + 1).start()
-
-            if j == n_blocks - 1:
-                @pl.when(k < n_chunks - 1)
-                def _():
-                    peer_copy(k + 1).wait_recv()
-                    forward_copy(k + 1).wait_recv()
-
-            logits(j, xslot, j % 2)
+            logits(j)
             if j:
-                state = epilogue(j - 1, (j - 1) % 2, want, state)
-            if j == n_blocks - 1:
-                normalise(lax.min(k + 1, n_chunks - 1), 1 - xslot)
-        state = epilogue(n_blocks - 1, (n_blocks - 1) % 2, want, state)
-        finish_chunk(k, state)
-        for n in range(3):
-            stat_copy(n, k).start()
-        return carry
-
-    lax.fori_loop(0, n_chunks, step, 0)
+                state = epilogue(j - 1, want, state)
+            else:
+                finish_chunk(lax.rem(k + n_chunks, n_chunks + 1), epilogue(final, last_want, last_state))
+        return (want, *state)
+
+    blank = jnp.zeros((8, chunk), jnp.float32)
+    zbuf[final % 2, 0 : v_local - starts[final], :] = jnp.zeros((v_local - starts[final], chunk), jnp.float32)
+    want, *state = lax.fori_loop(0, n_chunks, step, (jnp.full((8, chunk), -1, jnp.int32), blank, blank, blank))
+    send_stats(n_chunks - 2)
+    with ns("last"):
+        finish_chunk(n_chunks - 1, epilogue(final, want, state))
+    send_stats(n_chunks - 1)
 
     for k in range(n_chunks):
-        for n in range(3):
-            stat_copy(n, k).wait_recv()
+        with ns("statwait"):
+            for n in range(3):
+                stat_copy(n, k).wait_recv()
         stats = [stx[k]] + [srx[n, k] for n in range(3)]
         top = stats[0][0:1]
         for st in stats[1:]:
@@ -222,7 +238,10 @@
     for k in range(n_chunks):
         cross_copy(k).wait_send()
         peer_copy(k).wait_send()
-        forward_copy(k).wait_send()
+        if k:
+            diag_copy(k).wait_send()
+        else:
+            forward_copy().wait_send()
         for n in range(3):
             stat_copy(n, k).wait_send()
     for n in range(3):
@@ -251,9 +270,9 @@
                 pltpu.VMEM((4, 1, d_local), f32),
                 pltpu.VMEM((b, l), jnp.int32),
                 pltpu.VMEM((4 * d_local, LANES), f32),
-                pltpu.VMEM((2, 4 * d_local, chunk), jnp.bfloat16),
+                pltpu.VMEM((4 * d_local, chunk), jnp.bfloat16),
                 pltpu.VMEM((2, block, chunk), f32),
-                pltpu.VMEM((n_chunks, 8, chunk), f32),
+                pltpu.VMEM((n_chunks + 1, 8, chunk), f32),
                 pltpu.VMEM((3, n_chunks, 8, chunk), f32),
                 dma((len(w_parts),)),
                 dma((n_chunks,)),

time: 31.4 us -> 29.1 us (0.927)
  Pallas kernels: 29.4 us -> 27.1 us
    pallas_call x1, Pallas kernels: 29.4 us -> 27.1 us  [local_score(): pl.pallas_call(functools.partial(head_kernel, (d_local, v_local, rows, ch...]
where the time goes in v4:
time: 29.1 us; the launch traced here: 29 us
  Pallas kernels  27.1 us (93%)
  other arithmetic  1.22 us (4%)
  between operations  0.65 us (2%)
    pallas_call x1, Pallas kernels, local_score(): pl.pallas_call(functools.partial(head_kernel, (d_local, v_local, rows, ch...  27.1 us
    reduce_sum x1, other arithmetic, local_score(): return (token_logp, jnp.sum(token_logp, axis=1))  1.22 us

profile of v4, /device:TPU:0, one launch (start us, length us, event | category | flops | bytes accessed | tf_op | source)
XLA Modules:
  0.0 29.0 jit_solution(5185594415040705311)
XLA Ops:
  0.6 0.0 copy-start
  0.6 27.1 %shard_map.68 = f32[2,512]{1,0:T(2,128)S(1)} custom-call(bf16[2,192,512]{2,1,0:T(8,128)(2,1)} %bitcast.4, f32[1,192]{1,0:T(1,128)} %bitcast.5, bf16[8032,768]{1,0:T(8,128)(2,1)} %bitcast.3, s32[2,512]{1,0:T(2,128)} %tgt_ref.1), custom_call_target="tpu_custom_call" | custom-call | tf_op jit(solution)/shard_map/pallas_call | solution.py:262
  27.7 0.0 copy-done
  27.7 1.2 %fusion = (f32[2]{0:T(128)}, f32[2,512]{1,0:T(2,128)}) fusion(f32[2,512]{1,0:T(2,128)S(1)} %shard_map.68, s32[2,512]{1,0:T(2,128)S(1)} %copy-done), kind=kLoop, calls=%fused_computation.1 | loop fusion | flops 3070 | bytes 12296 | tf_op jit(solution)/shard_map/reduce_sum | solution.py:294
Async XLA Ops:
  0.6 27.1 %copy-start = (s32[2,512]{1,0:T(2,128)S(1)}, s32[2,512]{1,0:T(2,128)}, u32[]{:S(2)}) copy-start(s32[2,512]{1,0:T(2,128)} %param.9) | copy-start | bytes 12292

commit v5 on v4

--- a/solution.py
+++ b/solution.py
@@ -52,27 +52,42 @@
         own[k].start()
     own_t.start()
 
+    ns = jax.named_scope
     barrier = pltpu.get_barrier_semaphore()
     for other in others:
         pl.semaphore_signal(barrier, inc=1, device_id={"tp": other}, device_id_type=MESH)
-    pl.semaphore_wait(barrier, 3)
+    with ns("own"):
+        own_g.wait()
+        for k in range(n_chunks):
+            own[k].wait()
+        own_t.wait()
+        for part in load_w:
+            part.start()
+    with ns("barrier"):
+        pl.semaphore_wait(barrier, 3)
 
     def remote(src, dst, send, recv, dev):
         return pltpu.make_async_remote_copy(
             src_ref=src, dst_ref=dst, send_sem=send, recv_sem=recv, device_id={"tp": dev}, device_id_type=MESH
         )
 
-    def cross_copy(k):
-        return remote(piece(me, k), piece(me, k), xsend.at[k], xrecv.at[k], cross)
+    def part_of(owner, k, h):
+        if h is None:
+            return piece(owner, k)
+        return hrx.at[k, pl.ds(pl.multiple_of(owner * d_local, d_local), d_local), pl.ds(h * LANES, LANES)]
+
+    def cross_copy(k, h):
+        slot = 0 if h is None else h
+        return remote(part_of(me, k, h), part_of(me, k, h), xsend.at[slot, k], xrecv.at[slot, k], cross)
 
     def peer_copy(k):
         return remote(piece(me, k), piece(me, k), psend.at[k], precv.at[k], peer)
 
     def diag_copy(k):
-        return remote(piece(me, k), piece(me, k), fsend.at[k], frecv.at[k], diag)
-
-    def forward_copy():
-        return remote(piece(cross, 0), piece(cross, 0), fsend.at[0], frecv.at[0], peer)
+        return remote(part_of(me, k, 1), part_of(me, k, 1), fsend.at[1, k], frecv.at[1, k], diag)
+
+    def forward_copy(k, h):
+        return remote(part_of(cross, k, h), part_of(cross, k, h), fsend.at[0, k], frecv.at[0, k], peer)
 
     def gain_copy(n):
         return remote(grx.at[me], grx.at[me], gsend.at[n], grecv.at[n], others[n])
@@ -80,20 +95,17 @@
     def stat_copy(n, k):
         return remote(stx.at[k], srx.at[n, k], ssend.at[n, k], srecv.at[n, k], others[n])
 
-    ns = jax.named_scope
-    with ns("own"):
-        own_g.wait()
-        for n in range(3):
-            gain_copy(n).start()
-        for k in range(n_chunks):
-            own[k].wait()
-            cross_copy(k).start()
-            peer_copy(k).start()
-            if k:
-                diag_copy(k).start()
-        for part in load_w:
-            part.start()
-        own_t.wait()
+    for n in range(3):
+        gain_copy(n).start()
+    cross_copy(0, None).start()
+    for k in range(n_chunks):
+        peer_copy(k).start()
+    with ns("peer0"):
+        peer_copy(0).wait_recv()
+    for k in range(1, n_chunks):
+        cross_copy(k, 0).start()
+        cross_copy(k, 1).start()
+        diag_copy(k).start()
 
     for n in range(3):
         gain_copy(n).wait_recv()
@@ -127,17 +139,20 @@
 
     sub = lax.broadcasted_iota(jnp.int32, (8, chunk), 0)
 
+    def slot_of(j):
+        return j % 2 if j < n_blocks - 2 else 2 + j % 2
+
     def logits(j):
         lo = starts[j]
         size = min(block, v_local - lo)
-        zbuf[j % 2, 0:size, :] = jnp.dot(wbuf[lo : lo + size, :], xbuf[...], preferred_element_type=jnp.float32)
+        zbuf[slot_of(j), 0:size, :] = jnp.dot(wbuf[lo : lo + size, :], xbuf[...], preferred_element_type=jnp.float32)
 
     def epilogue(j, want, state):
         lo = starts[j]
         size = min(block, v_local - lo)
 
         def tile(i):
-            return zbuf[j % 2, pl.ds(pl.multiple_of(i * 8, 8), 8), :]
+            return zbuf[slot_of(j), pl.ds(pl.multiple_of(i * 8, 8), 8), :]
 
         top = lax.fori_loop(1, size // 8, lambda i, t: jnp.maximum(t, tile(i)), tile(0), unroll=True)
         if state is None:
@@ -166,11 +181,10 @@
         stx[k, 2:3, :] = jnp.sum(pick, axis=0, keepdims=True)
 
     with ns("cross0"):
-        cross_copy(0).wait_recv()
-    forward_copy().start()
+        cross_copy(0, None).wait_recv()
+    forward_copy(0, None).start()
     with ns("fwd0"):
-        peer_copy(0).wait_recv()
-        forward_copy().wait_recv()
+        forward_copy(0, None).wait_recv()
     with ns("wwait"):
         for part in load_w:
             part.wait()
@@ -191,9 +205,16 @@
         @pl.when(k > 0)
         def _():
             with ns("chunkwait"):
-                cross_copy(k).wait_recv()
+                forward_copy(k, 0).wait_recv()
+                cross_copy(k, 1).wait_recv()
                 peer_copy(k).wait_recv()
                 diag_copy(k).wait_recv()
+
+        @pl.when(k < n_chunks - 1)
+        def _():
+            with ns("halfwait"):
+                cross_copy(k + 1, 0).wait_recv()
+            forward_copy(k + 1, 0).start()
 
         @pl.when(k > 1)
         def _():
@@ -205,18 +226,20 @@
         state = None
         for j in range(n_blocks):
             logits(j)
-            if j:
+            if j == 0:
+                last_state = epilogue(final - 1, last_want, last_state)
+                finish_chunk(lax.rem(k + n_chunks, n_chunks + 1), epilogue(final, last_want, last_state))
+            elif j < final:
                 state = epilogue(j - 1, want, state)
-            else:
-                finish_chunk(lax.rem(k + n_chunks, n_chunks + 1), epilogue(final, last_want, last_state))
         return (want, *state)
 
     blank = jnp.zeros((8, chunk), jnp.float32)
-    zbuf[final % 2, 0 : v_local - starts[final], :] = jnp.zeros((v_local - starts[final], chunk), jnp.float32)
+    for j in (final - 1, final):
+        zbuf[slot_of(j), 0 : min(block, v_local - starts[j]), :] = jnp.zeros((min(block, v_local - starts[j]), chunk), jnp.float32)
     want, *state = lax.fori_loop(0, n_chunks, step, (jnp.full((8, chunk), -1, jnp.int32), blank, blank, blank))
     send_stats(n_chunks - 2)
     with ns("last"):
-        finish_chunk(n_chunks - 1, epilogue(final, want, state))
+        finish_chunk(n_chunks - 1, epilogue(final, want, epilogue(final - 1, want, state)))
     send_stats(n_chunks - 1)
 
     for k in range(n_chunks):
@@ -236,12 +259,12 @@
         out_ref[seq : seq + 1, pos : pos + chunk] = pick - (top + jnp.log(total))
 
     for k in range(n_chunks):
-        cross_copy(k).wait_send()
         peer_copy(k).wait_send()
+        forward_copy(k, 0 if k else None).wait_send()
+        cross_copy(k, 0 if k else None).wait_send()
         if k:
+            cross_copy(k, 1).wait_send()
             diag_copy(k).wait_send()
-        else:
-            forward_copy().wait_send()
         for n in range(3):
             stat_copy(n, k).wait_send()
     for n in range(3):
@@ -271,15 +294,15 @@
                 pltpu.VMEM((b, l), jnp.int32),
                 pltpu.VMEM((4 * d_local, LANES), f32),
                 pltpu.VMEM((4 * d_local, chunk), jnp.bfloat16),
-                pltpu.VMEM((2, block, chunk), f32),
+                pltpu.VMEM((4, block, chunk), f32),
                 pltpu.VMEM((n_chunks + 1, 8, chunk), f32),
                 pltpu.VMEM((3, n_chunks, 8, chunk), f32),
                 dma((len(w_parts),)),
                 dma((n_chunks,)),
                 dma((2,)),
                 dma((n_chunks,)), dma((n_chunks,)),
-                dma((n_chunks,)), dma((n_chunks,)),
-                dma((n_chunks,)), dma((n_chunks,)),
+                dma((2, n_chunks)), dma((2, n_chunks)),
+                dma((2, n_chunks)), dma((2, n_chunks)),
                 dma((3,)), dma((3,)),
                 dma((3, n_chunks)), dma((3, n_chunks)),
             ],

time: 29.1 us -> 29.2 us (level)
  no operation moved by 1% of the time
where the time goes in v5:
time: 29.2 us; the launch traced here: 29.1 us
  Pallas kernels  27.2 us (93%)
  other arithmetic  1.22 us (4%)
  between operations  0.65 us (2%)
    pallas_call x1, Pallas kernels, local_score(): pl.pallas_call(functools.partial(head_kernel, (d_local, v_local, rows, ch...  27.2 us
    reduce_sum x1, other arithmetic, local_score(): return (token_logp, jnp.sum(token_logp, axis=1))  1.22 us

profile of v5, /device:TPU:0, one launch (start us, length us, event | category | flops | bytes accessed | tf_op | source)
XLA Modules:
  0.0 29.1 jit_solution(9830405694965978155)
XLA Ops:
  0.6 0.0 copy-start
  0.6 27.2 %shard_map.68 = f32[2,512]{1,0:T(2,128)S(1)} custom-call(bf16[2,192,512]{2,1,0:T(8,128)(2,1)} %bitcast.4, f32[1,192]{1,0:T(1,128)} %bitcast.5, bf16[8032,768]{1,0:T(8,128)(2,1)} %bitcast.3, s32[2,512]{1,0:T(2,128)} %tgt_ref.1), custom_call_target="tpu_custom_call" | custom-call | tf_op jit(solution)/shard_map/pallas_call | solution.py:285
  27.8 0.0 copy-done
  27.8 1.2 %fusion = (f32[2]{0:T(128)}, f32[2,512]{1,0:T(2,128)}) fusion(f32[2,512]{1,0:T(2,128)S(1)} %shard_map.68, s32[2,512]{1,0:T(2,128)S(1)} %copy-done), kind=kLoop, calls=%fused_computation.1 | loop fusion | flops 3070 | bytes 12296 | tf_op jit(solution)/shard_map/reduce_sum | solution.py:317
Async XLA Ops:
  0.6 27.2 %copy-start = (s32[2,512]{1,0:T(2,128)S(1)}, s32[2,512]{1,0:T(2,128)}, u32[]{:S(2)}) copy-start(s32[2,512]{1,0:T(2,128)} %param.9) | copy-start | bytes 12292
